TPU v7x, 32 devices: a whole 2x2x4 slice. The times are simulated.
32 devices in a mesh: seq: 16 (over z, y, core), tp: 2 (over x).
Axes of the slice: x: 2, y: 2, z: 4, core: 2. Of those that a mesh axis runs over, the one named last changes fastest.
Arguments:
- tokens: bfloat16 [16384, 1024], P('seq'), may hold values from -6 to 6
- cotangent: bfloat16 [16384, 1024], P('seq'), may hold values from -6 to 6
- mem_keys: bfloat16 [131072, 1024], P('seq', 'tp'), may hold values from -6 to 6
- mem_values: bfloat16 [131072, 1024], P('seq', 'tp'), may hold values from -6 to 6
- doc_ids: int32 [16, 1024], P('seq'), may hold values from 0 to 3, never falling along the last dimension, each value on 1 to 512 neighbouring positions
- mem_len: int32 [16], P('seq'), may hold values from 1 to 8192, 65536 in all
- owner_perm: int32 [32], replicated, may hold values from 0 to 31, each once
- gain_w: float32 [2, 1024], P(None, 'seq'), may hold values from 0.5 to 1.5
- gain_m: float32 [2, 1024], P(None, 'seq'), may hold values from -96 to 96
- gain_v: float32 [2, 1024], P(None, 'seq'), may hold values from 100 to 10000
- attn_w: float32 [4, 8, 32, 32, 128], P(None, 'tp', 'seq')
- attn_m: float32 [4, 8, 32, 32, 128], P(None, 'tp', 'seq')
- attn_v: float32 [4, 8, 32, 32, 128], P(None, 'tp', 'seq')
- attn_left: float32 [4, 8, 32, 32, 32], P(None, 'tp', 'seq')
- attn_right: float32 [4, 8, 32, 128, 128], P(None, 'tp', 'seq')
- mlp_w: float32 [3, 8, 32, 32, 352], P(None, 'tp', 'seq')
- mlp_m: float32 [3, 8, 32, 32, 352], P(None, 'tp', 'seq'), may hold values from -48 to 48
- mlp_v: float32 [3, 8, 32, 32, 352], P(None, 'tp', 'seq'), may hold values from 30 to 3000
- mlp_left: float32 [3, 8, 32, 32, 32], P(None, 'tp', 'seq')
- mlp_right: float32 [3, 8, 32, 352, 352], P(None, 'tp', 'seq')
Outputs:
- block_out: float32 [16384, 1024], P('seq')
- input_grad: float32 [16384, 1024], P('seq')
- new_keys: bfloat16 [16384, 1024], P('seq', 'tp')
- new_values: bfloat16 [16384, 1024], P('seq', 'tp')
- attn_grad: float32 [4, 8, 32, 32, 128], P(None, 'tp', 'seq')
- mlp_grad: float32 [3, 8, 32, 32, 352], P(None, 'tp', 'seq')
- gain_grad: float32 [2, 1024], P(None, 'seq')
- attn_update: float32 [4, 8, 32, 32, 128], P(None, 'tp', 'seq')
- attn_new_m: float32 [4, 8, 32, 32, 128], P(None, 'tp', 'seq')
- attn_new_v: float32 [3, 8, 32, 32, 128], P(None, 'tp', 'seq')
- out_new_v: float32 [8, 32, 32, 128], P('tp', 'seq')
- mlp_new_w: float32 [3, 8, 32, 32, 352], P(None, 'tp', 'seq')
- mlp_new_m: float32 [3, 8, 32, 32, 352], P(None, 'tp', 'seq')
- mlp_new_v: float32 [3, 8, 32, 32, 352], P(None, 'tp', 'seq')
- gain_update: float32 [2, 1024], P(None, 'seq')
- gain_new_m: float32 [2, 1024], P(None, 'seq')
- gain_new_v: float32 [2, 1024], P(None, 'seq')
Inputs may be any that keep to these rules, and one draw needn't show every extreme that they name: `doc_ids`: document ids of each segment start at 0 and never fall along the segment. `mem_len`: live memory slots of each segment, the first ones of its cache. `owner_perm`: each row block number stands once.
All inputs are finite; a program needn't handle non-finite values. No bound on the sum of `mem_len` on one device may be relied on, other than what follows from the above.
Results may differ from a plain program's by a relative error of at most 0.018.
The roundings to bfloat16 on the way count: a program that leaves them out, or rounds other values in their place, can miss the bound.
Values may be sent and summed in bfloat16 or wider, within the bound.
A program may use at most 256 MiB of HBM per device.

v0:
```python
import jax
import jax.numpy as jnp
from jax import lax
from jax.sharding import PartitionSpec as P

norm_eps = 1e-06
adam_eps = 1e-08
beta_one = 0.9
beta_two = 0.95
learn_rate = 0.01
gain_rate = 0.02
corr_first = 1.0 - 0.9**10
corr_second = 1.0 - 0.95**10
masked_out = -1e30
highest = lax.Precision.HIGHEST


def to_matrix(blocks):
    groups, block_count, height, block_width = blocks.shape
    return jnp.transpose(blocks, (1, 2, 0, 3)).reshape(block_count * height, groups * block_width)


def from_matrix(matrix, groups, row_blocks):
    total_rows, total_cols = matrix.shape
    shaped = matrix.reshape(row_blocks, total_rows // row_blocks, groups, total_cols // groups)
    return jnp.transpose(shaped, (2, 0, 1, 3))


def norm_forward(values, gain_row):
    factor = lax.rsqrt(jnp.mean(values * values, axis=-1, keepdims=True) + norm_eps)
    return (values * factor * gain_row, factor)


def norm_backward(values, factor, gain_row, grad_normed):
    scaled = grad_normed * gain_row
    inner_mean = jnp.mean(scaled * values, axis=-1, keepdims=True)
    grad_values = factor * scaled - values * (factor * factor * factor) * inner_mean
    grad_gain = jnp.sum(grad_normed * values * factor, axis=0)
    return (grad_values, grad_gain)


def own_scores(block_queries, keys_own, doc_row, query_docs, start, scale):
    scores = (
        jnp.einsum("qhd,khd->hqk", block_queries, keys_own, preferred_element_type=jnp.float32)
        * scale
    )
    positions = start + jnp.arange(block_queries.shape[0], dtype=jnp.int32)
    columns = jnp.arange(keys_own.shape[0], dtype=jnp.int32)
    keep_mask = (columns[None, :] <= positions[:, None]) & (doc_row[None, :] == query_docs[:, None])
    return jnp.where(keep_mask[None], scores, masked_out)


def memory_scores(block_queries, block_keys, sees_memory, live_count, step_index, scale):
    scores = (
        jnp.einsum("qhd,khd->hqk", block_queries, block_keys, preferred_element_type=jnp.float32)
        * scale
    )
    key_rows = block_keys.shape[0]
    memory_slots = step_index * key_rows + jnp.arange(key_rows, dtype=jnp.int32)
    keep_mask = sees_memory[:, None] & (memory_slots[None, :] < live_count)
    return jnp.where(keep_mask[None], scores, masked_out)


def attend_forward(
    queries, keys_own, values_own, memory_keys, memory_values, doc_row, live_count, scale
):
    seg_len = queries.shape[0]
    block_rows = min(512, seg_len)
    key_steps = jnp.arange(memory_keys.shape[0], dtype=jnp.int32)
    first_doc = doc_row[0]

    def one_block(start):
        block_queries = lax.dynamic_slice_in_dim(queries, start, block_rows, 0)
        query_docs = lax.dynamic_slice_in_dim(doc_row, start, block_rows, 0)
        sees_memory = query_docs == first_doc
        own_part = own_scores(block_queries, keys_own, doc_row, query_docs, start, scale)
        row_top = jnp.max(own_part, axis=-1)
        row_total = jnp.sum(jnp.exp(own_part - row_top[..., None]), axis=-1)

        def gather_stats(state_pair, step_item):
            running_top, running_total = state_pair
            block_keys, step_index = step_item
            scores = memory_scores(
                block_queries, block_keys, sees_memory, live_count, step_index, scale
            )
            fresh_top = jnp.maximum(running_top, jnp.max(scores, axis=-1))
            fresh_total = running_total * jnp.exp(running_top - fresh_top) + jnp.sum(
                jnp.exp(scores - fresh_top[..., None]), axis=-1
            )
            return ((fresh_top, fresh_total), None)

        (row_top, row_total), _ = lax.scan(
            gather_stats, (row_top, row_total), (memory_keys, key_steps)
        )
        log_total = row_top + jnp.log(row_total)
        own_weights = jnp.exp(own_part - log_total[..., None]).astype(jnp.bfloat16)
        output = jnp.einsum(
            "hqk,khd->qhd", own_weights, values_own, preferred_element_type=jnp.float32
        )

        def add_values(running_sum, step_item):
            block_keys, block_values, step_index = step_item
            scores = memory_scores(
                block_queries, block_keys, sees_memory, live_count, step_index, scale
            )
            block_weights = jnp.exp(scores - log_total[..., None]).astype(jnp.bfloat16)
            return (
                running_sum
                + jnp.einsum(
                    "hqk,khd->qhd", block_weights, block_values, preferred_element_type=jnp.float32
                ),
                None,
            )

        output, _ = lax.scan(add_values, output, (memory_keys, memory_values, key_steps))
        return (output, log_total)

    starts = jnp.arange(seg_len // block_rows, dtype=jnp.int32) * block_rows
    outputs, log_totals = lax.map(one_block, starts)
    return (outputs.reshape(queries.shape), (starts, log_totals))


def attend_backward(
    queries,
    keys_own,
    values_own,
    memory_keys,
    memory_values,
    doc_row,
    live_count,
    scale,
    grad_output,
    kept_stats,
):
    seg_len = queries.shape[0]
    block_rows = min(512, seg_len)
    key_steps = jnp.arange(memory_keys.shape[0], dtype=jnp.int32)
    first_doc = doc_row[0]

    def one_block(state_pair, block_item):
        grad_keys_sum, grad_values_sum = state_pair
        start, log_total = block_item
        block_queries = lax.dynamic_slice_in_dim(queries, start, block_rows, 0)
        block_grads = lax.dynamic_slice_in_dim(grad_output, start, block_rows, 0)
        query_docs = lax.dynamic_slice_in_dim(doc_row, start, block_rows, 0)
        sees_memory = query_docs == first_doc
        own_part = own_scores(block_queries, keys_own, doc_row, query_docs, start, scale)
        own_weights = jnp.exp(own_part - log_total[..., None])
        own_dprob = jnp.einsum(
            "qhd,khd->hqk", block_grads, values_own, preferred_element_type=jnp.float32
        )
        delta = jnp.sum(own_weights * own_dprob, axis=-1)

        def delta_step(delta_sum, step_item):
            block_keys, block_values, step_index = step_item
            scores = memory_scores(
                block_queries, block_keys, sees_memory, live_count, step_index, scale
            )
            block_weights = jnp.exp(scores - log_total[..., None])
            block_dprob = jnp.einsum(
                "qhd,khd->hqk", block_grads, block_values, preferred_element_type=jnp.float32
            )
            return (delta_sum + jnp.sum(block_weights * block_dprob, axis=-1), None)

        delta, _ = lax.scan(delta_step, delta, (memory_keys, memory_values, key_steps))
        own_dscore = (own_weights * (own_dprob - delta[..., None])).astype(jnp.bfloat16)
        grad_queries = jnp.einsum(
            "hqk,khd->qhd", own_dscore, keys_own, preferred_element_type=jnp.float32
        )
        grad_keys_sum = grad_keys_sum + jnp.einsum(
            "hqk,qhd->khd", own_dscore, block_queries, preferred_element_type=jnp.float32
        )
        grad_values_sum = grad_values_sum + jnp.einsum(
            "hqk,qhd->khd",
            own_weights.astype(jnp.bfloat16),
            block_grads,
            preferred_element_type=jnp.float32,
        )

        def grad_step(query_sum, step_item):
            block_keys, block_values, step_index = step_item
            scores = memory_scores(
                block_queries, block_keys, sees_memory, live_count, step_index, scale
            )
            block_weights = jnp.exp(scores - log_total[..., None])
            block_dprob = jnp.einsum(
                "qhd,khd->hqk", block_grads, block_values, preferred_element_type=jnp.float32
            )
            block_dscore = (block_weights * (block_dprob - delta[..., None])).astype(jnp.bfloat16)
            return (
                query_sum
                + jnp.einsum(
                    "hqk,khd->qhd", block_dscore, block_keys, preferred_element_type=jnp.float32
                ),
                None,
            )

        grad_queries, _ = lax.scan(grad_step, grad_queries, (memory_keys, memory_values, key_steps))
        return ((grad_keys_sum, grad_values_sum), grad_queries * scale)

    empty = jnp.zeros(keys_own.shape, jnp.float32)
    (grad_keys, grad_values), grad_blocks = lax.scan(one_block, (empty, empty), kept_stats)
    return (grad_blocks.reshape(queries.shape), grad_keys * scale, grad_values)


def rotate_step(grad, first, second, left_basis, right_basis):
    turned = jnp.einsum("...ji,...jk->...ik", left_basis, grad, precision=highest)
    turned = jnp.einsum("...ik,...kl->...il", turned, right_basis, precision=highest)
    first = beta_one * first + (1.0 - beta_one) * turned
    second = beta_two * second + (1.0 - beta_two) * turned * turned
    direction = first / corr_first / (jnp.sqrt(second / corr_second) + adam_eps)
    turned_back = jnp.einsum("...ij,...jk->...ik", left_basis, direction, precision=highest)
    turned_back = jnp.einsum("...ik,...lk->...il", turned_back, right_basis, precision=highest)
    return (-(learn_rate * turned_back), first, second)


def adam_step(grad, first, second):
    first = beta_one * first + (1.0 - beta_one) * grad
    second = beta_two * second + (1.0 - beta_two) * grad * grad
    direction = first / corr_first / (jnp.sqrt(second / corr_second) + adam_eps)
    return (-(gain_rate * direction), first, second)


def on_device(
    tokens,
    cotangent,
    mem_keys,
    mem_values,
    doc_ids,
    mem_len,
    owner_perm,
    gain_w,
    gain_m,
    gain_v,
    attn_w,
    attn_m,
    attn_v,
    attn_left,
    attn_right,
    mlp_w,
    mlp_m,
    mlp_v,
    mlp_left,
    mlp_right,
):
    attn_stored, mlp_stored = (
        lax.all_gather(attn_w.astype(jnp.bfloat16), "seq", axis=2, tiled=True),
        lax.all_gather(mlp_w.astype(jnp.bfloat16), "seq", axis=2, tiled=True),
    )
    gain_pair = lax.all_gather(gain_w, "seq", axis=1, tiled=True)
    block_total = owner_perm.shape[0]
    inverse = (
        jnp.zeros((block_total,), jnp.int32)
        .at[owner_perm]
        .set(jnp.arange(block_total, dtype=jnp.int32))
    )
    attn_low = attn_stored[:, :, inverse]
    mlp_low = mlp_stored[:, :, inverse]
    head_count = attn_w.shape[1]
    head_size = attn_w.shape[4]
    group_count = mlp_w.shape[1]
    scale = head_size ** (-0.5)
    weight_qkv = jnp.concatenate(
        [to_matrix(attn_low[0]), to_matrix(attn_low[1]), to_matrix(attn_low[2])], axis=1
    )
    weight_out = to_matrix(attn_low[3])
    weight_gu = jnp.concatenate([to_matrix(mlp_low[0]), to_matrix(mlp_low[1])], axis=1)
    weight_down = to_matrix(mlp_low[2])
    width_heads = head_count * head_size
    width_hidden = weight_down.shape[1]
    seg_len = tokens.shape[0]
    doc_row = doc_ids[0]
    live_count = mem_len[0]
    key_rows = min(2048, mem_keys.shape[0])
    memory_keys = mem_keys.reshape(mem_keys.shape[0] // key_rows, key_rows, head_count, head_size)
    memory_values = mem_values.reshape(
        mem_values.shape[0] // key_rows, key_rows, head_count, head_size
    )
    resid_in = tokens.astype(jnp.float32)
    normed_one, factor_one = norm_forward(resid_in, gain_pair[0])
    acts_one = normed_one.astype(jnp.bfloat16)
    projected = jnp.dot(acts_one, weight_qkv, preferred_element_type=jnp.float32).astype(
        jnp.bfloat16
    )
    queries = projected[:, :width_heads].reshape(seg_len, head_count, head_size)
    keys_new = projected[:, width_heads : 2 * width_heads]
    values_new = projected[:, 2 * width_heads :]
    keys_heads = keys_new.reshape(seg_len, head_count, head_size)
    values_heads = values_new.reshape(seg_len, head_count, head_size)
    attended, kept_stats = attend_forward(
        queries, keys_heads, values_heads, memory_keys, memory_values, doc_row, live_count, scale
    )
    mixed_heads = attended.reshape(seg_len, width_heads).astype(jnp.bfloat16)
    partial_attn = jnp.einsum(
        "tc,dc->td", mixed_heads, weight_out, preferred_element_type=jnp.float32
    )
    attn_out = lax.psum(partial_attn, "tp")
    hidden_state = resid_in + attn_out
    normed_two, factor_two = norm_forward(hidden_state, gain_pair[1])
    acts_two = normed_two.astype(jnp.bfloat16)
    gate_up = jnp.dot(acts_two, weight_gu, preferred_element_type=jnp.float32)
    gate_val = gate_up[:, :width_hidden]
    up_val = gate_up[:, width_hidden:]
    sigmoid_gate = jax.nn.sigmoid(gate_val)
    silu_gate = gate_val * sigmoid_gate
    inner_act = (silu_gate * up_val).astype(jnp.bfloat16)
    partial_mlp = jnp.einsum(
        "tf,df->td", inner_act, weight_down, preferred_element_type=jnp.float32
    )
    mlp_out = lax.psum(partial_mlp.astype(jnp.bfloat16), "tp").astype(jnp.float32)
    block_out = hidden_state + mlp_out
    grad_out = cotangent.astype(jnp.float32)
    grad_down = jnp.einsum("td,tf->df", cotangent, inner_act, preferred_element_type=jnp.float32)
    grad_inner = jnp.einsum("td,df->tf", cotangent, weight_down, preferred_element_type=jnp.float32)
    grad_gate = grad_inner * up_val * sigmoid_gate * (1.0 + gate_val * (1.0 - sigmoid_gate))
    grad_up = grad_inner * silu_gate
    grad_gu = jnp.concatenate([grad_gate, grad_up], axis=1).astype(jnp.bfloat16)
    grad_weight_gu = jnp.einsum("td,tf->df", acts_two, grad_gu, preferred_element_type=jnp.float32)
    partial_two = jnp.einsum("tf,df->td", grad_gu, weight_gu, preferred_element_type=jnp.float32)
    grad_normed_two = lax.psum(partial_two, "tp")
    grad_hidden_norm, grad_gain_two = norm_backward(
        hidden_state, factor_two, gain_pair[1], grad_normed_two
    )
    grad_hidden = grad_out + grad_hidden_norm
    mlp_grads = jnp.stack(
        [
            from_matrix(grad_weight_gu[:, :width_hidden], group_count, block_total),
            from_matrix(grad_weight_gu[:, width_hidden:], group_count, block_total),
            from_matrix(grad_down, group_count, block_total),
        ]
    )[:, :, owner_perm]
    grad_hidden_low = grad_hidden.astype(jnp.bfloat16)
    grad_out_weight = jnp.einsum(
        "td,tc->dc", grad_hidden_low, mixed_heads, preferred_element_type=jnp.float32
    )
    grad_mixed = jnp.einsum(
        "td,dc->tc", grad_hidden_low, weight_out, preferred_element_type=jnp.float32
    ).astype(jnp.bfloat16)
    grad_queries, grad_keys, grad_values = attend_backward(
        queries,
        keys_heads,
        values_heads,
        memory_keys,
        memory_values,
        doc_row,
        live_count,
        scale,
        grad_mixed.reshape(seg_len, head_count, head_size),
        kept_stats,
    )
    grad_projected = jnp.concatenate(
        [
            grad_queries.reshape(seg_len, width_heads),
            grad_keys.reshape(seg_len, width_heads),
            grad_values.reshape(seg_len, width_heads),
        ],
        axis=1,
    ).astype(jnp.bfloat16)
    grad_weight_qkv = jnp.einsum(
        "td,tc->dc", acts_one, grad_projected, preferred_element_type=jnp.float32
    )
    partial_one = jnp.einsum(
        "tc,dc->td", grad_projected, weight_qkv, preferred_element_type=jnp.float32
    )
    grad_normed_one = lax.psum(partial_one, "tp")
    grad_tokens_norm, grad_gain_one = norm_backward(
        resid_in, factor_one, gain_pair[0], grad_normed_one
    )
    input_grad = grad_hidden + grad_tokens_norm
    attn_grads = jnp.stack(
        [
            from_matrix(grad_weight_qkv[:, :width_heads], head_count, block_total),
            from_matrix(grad_weight_qkv[:, width_heads : 2 * width_heads], head_count, block_total),
            from_matrix(grad_weight_qkv[:, 2 * width_heads :], head_count, block_total),
            from_matrix(grad_out_weight, head_count, block_total),
        ]
    )[:, :, owner_perm]
    gain_grads = jnp.stack([grad_gain_one, grad_gain_two])
    attn_grad, mlp_grad, gain_grad = (
        lax.psum_scatter(attn_grads, "seq", scatter_dimension=2, tiled=True),
        lax.psum_scatter(mlp_grads, "seq", scatter_dimension=2, tiled=True),
        lax.psum_scatter(gain_grads, "seq", scatter_dimension=1, tiled=True),
    )
    attn_new = rotate_step(attn_grad, attn_m, attn_v, attn_left, attn_right)
    mlp_new = rotate_step(mlp_grad, mlp_m, mlp_v, mlp_left, mlp_right)
    gain_new = adam_step(gain_grad, gain_m, gain_v)
    return (
        block_out,
        input_grad,
        keys_new,
        values_new,
        attn_grad,
        mlp_grad,
        gain_grad,
        attn_new[0],
        attn_new[1],
        attn_new[2][:3],
        attn_new[2][3],
        mlp_w + mlp_new[0],
        mlp_new[1],
        mlp_new[2],
        gain_new[0],
        gain_new[1],
        gain_new[2],
    )


def solution(mesh):
    in_specs = (
        P("seq", None),
        P("seq", None),
        P("seq", "tp"),
        P("seq", "tp"),
        P("seq", None),
        P("seq"),
        P(),
        P(None, "seq"),
        P(None, "seq"),
        P(None, "seq"),
        P(None, "tp", "seq", None, None),
        P(None, "tp", "seq", None, None),
        P(None, "tp", "seq", None, None),
        P(None, "tp", "seq", None, None),
        P(None, "tp", "seq", None, None),
        P(None, "tp", "seq", None, None),
        P(None, "tp", "seq", None, None),
        P(None, "tp", "seq", None, None),
        P(None, "tp", "seq", None, None),
        P(None, "tp", "seq", None, None),
    )
    out_specs = (
        P("seq", None),
        P("seq", None),
        P("seq", "tp"),
        P("seq", "tp"),
        P(None, "tp", "seq", None, None),
        P(None, "tp", "seq", None, None),
        P(None, "seq"),
        P(None, "tp", "seq", None, None),
        P(None, "tp", "seq", None, None),
        P(None, "tp", "seq", None, None),
        P("tp", "seq", None, None),
        P(None, "tp", "seq", None, None),
        P(None, "tp", "seq", None, None),
        P(None, "tp", "seq", None, None),
        P(None, "seq"),
        P(None, "seq"),
        P(None, "seq"),
    )
    return jax.shard_map(
        on_device, mesh=mesh, in_specs=in_specs, out_specs=out_specs, check_vma=False
    )
```

profile of v0, /device:TPU:0, one launch (start us, length us, event | category | flops | bytes accessed | tf_op | source)
XLA Modules:
  0.0 1752.3 jit_solution(3992857990212748352)
XLA Ops:
  9.3 23.4 %all-gather = f32[16,64,2]{1,2,0:T(2,128)S(1)} all-gather(f32[1,64,2]{1,2,0:T(2,128)} %bitcast.480), channel_id=1, replica_groups=mesh['seq'=16,'tp'=2] {'seq'}, dimensions={0}, use_global_device_ids=true | all-gather | bytes 8704 | tf_op jit(solution)/shard_map/all_gather | solution.py:250
  105.6 229.5 %while.82 = (s32[]{:T(128)}, bf16[2,512,4,128]{1,3,2,0:T(8,128)(2,1)}, f32[2,4,512]{2,1,0:T(4,128)S(1)}, s32[2]{0:T(128)S(1)}, s32[1,1024]{1,0:T(1,128)S(1)}, /*...) while((s32[]{:T(128)}, ...), condition=%wide.region_11.12_spmd.clone.clone, body=%wide.region_2.11_spmd.clone.clone.sunk | while | flops 4368116736 | bytes 118171888 | solution.py:119
  118.6 43.4 %while.86 = (s32[]{:T(128)}, f32[4,512]{1,0:T(4,128)S(1)}, f32[4,512]{1,0:T(4,128)S(1)}, pred[512]{0:T(512)(128)(4,1)S(1)}, s32[4]{0:T(128)S(1)}, /*index=5*/s32...) while((s32[]{:T(128)}, f32[4,512]{1,0:T(4,128)S(1)}, ...), condition=%wide.region_8.8_spmd, body=%wide.region_5.7_spmd.sunk | while | flops 1104158720 | bytes 39433348 | solution.py:92
  171.3 46.9 %while.87 = (s32[]{:T(128)}, f32[512,4,128]{0,2,1:T(8,128)}, bf16[4,2048,4,128]{1,3,2,0:T(8,128)(2,1)}, pred[512]{0:T(512)(128)(4,1)S(1)}, s32[4]{0:T(128)S(1)},...) while((s32[]{:T(128)}, f32[512,4,128]{0,2,1:T(8,128)}, ...), condition=%wide.region_10.10_spmd, body=%wide.region_9.9_spmd.sunk | while | flops 2165575680 | bytes 8926861 | solution.py:115
  233.1 43.4 %while.86 = (s32[]{:T(128)}, f32[4,512]{1,0:T(4,128)S(1)}, f32[4,512]{1,0:T(4,128)S(1)}, pred[512]{0:T(512)(128)(4,1)S(1)}, s32[4]{0:T(128)S(1)}, /*index=5*/s32...) while((s32[]{:T(128)}, f32[4,512]{1,0:T(4,128)S(1)}, ...), condition=%wide.region_8.8_spmd, body=%wide.region_5.7_spmd.sunk | while | flops 1104158720 | bytes 39433348 | solution.py:92
  285.7 46.9 %while.87 = (s32[]{:T(128)}, f32[512,4,128]{0,2,1:T(8,128)}, bf16[4,2048,4,128]{1,3,2,0:T(8,128)(2,1)}, pred[512]{0:T(512)(128)(4,1)S(1)}, s32[4]{0:T(128)S(1)},...) while((s32[]{:T(128)}, f32[512,4,128]{0,2,1:T(8,128)}, ...), condition=%wide.region_10.10_spmd, body=%wide.region_9.9_spmd.sunk | while | flops 2165575680 | bytes 8926861 | solution.py:115
  345.5 103.1 %all-reduce.5.cloned.1.call-done = f32[1024,1024]{1,0:T(8,128)} async-done(((f32[1024,1024]{1,0:T(8,128)}), f32[1024,1024]{1,0:T(8,128)}) %all-reduce.5.cloned.1.call-update) | async-done | bytes 4194320 | tf_op jit(solution)/shard_map/psum | solution.py:297
  454.0 78.4 %all-gather.6.cloned.1.call-done = bf16[3,4,32,32,352]{4,3,2,1,0:T(8,128)(2,1)} async-done(((bf16[3,4,2,32,352]{4,3,2,1,0:T(8,128)(2,1)}), bf16[3,4,32,32,352]{4,3,2,1,0:T(8,128)(2,1)}) %all-gather.6.cloned.1.call-update) | async-done | bytes 8650768 | tf_op jit(solution)/shard_map/all_gather | solution.py:248
  633.9 90.6 %all-reduce.9.cloned.1.call-done = f32[1024,1024]{1,0:T(8,128)} async-done(((f32[1024,1024]{1,0:T(8,128)}), f32[1024,1024]{1,0:T(8,128)}) %all-reduce.9.cloned.1.call-update) | async-done | bytes 4194320 | tf_op jit(solution)/shard_map/psum | solution.py:320
  729.6 60.0 %all-reduce.7.cloned.1.call-done = bf16[1024,1024]{1,0:T(8,128)(2,1)} async-done(((bf16[1024,1024]{1,0:T(8,128)(2,1)}), bf16[1024,1024]{1,0:T(8,128)(2,1)}) %all-reduce.7.cloned.1.call-update) | async-done | bytes 2097168 | tf_op jit(solution)/shard_map/psum | solution.py:310
  802.3 422.5 %while.85 = (s32[]{:T(128)}, f32[1024,4,128]{0,2,1:T(8,128)}, f32[1024,4,128]{0,2,1:T(8,128)}, bf16[2,512,4,128]{1,3,2,0:T(8,128)(2,1)}, s32[2]{0:T(128)S(1)}, /...) while((s32[]{:T(128)}, f32[1024,4,128]{0,2,1:T(8,128)}, ...), condition=%wide.region_24.25_spmd.clone.clone, body=%wide.region_17.24_spmd.clone.clone.sunk | while | flops 8136956928 | bytes 240430896 | solution.py:202
  818.7 53.4 %while.88 = (s32[]{:T(128)}, f32[4,512]{1,0:T(4,128)S(1)}, pred[512]{0:T(512)(128)(4,1)S(1)}, s32[4]{0:T(128)S(1)}, s32[]{:T(128)}, /*index=5*/bf16[4,2048,4,128...) while((s32[]{:T(128)}, f32[4,512]{1,0:T(4,128)S(1)}, ...), condition=%wide.region_21.21_spmd, body=%wide.region_19.20_spmd.sunk | while | flops 2169507840 | bytes 40941204 | solution.py:165
  887.4 111.6 %while.89 = (s32[]{:T(128)}, f32[512,4,128]{0,2,1:T(8,128)}, bf16[4,2048,4,128]{3,1,2,0:T(8,128)(2,1)}, pred[512]{0:T(512)(128)(4,1)S(1)}, s32[4]{0:T(128)S(1)},...) while((s32[]{:T(128)}, f32[512,4,128]{0,2,1:T(8,128)}, ...), condition=%wide.region_23.23_spmd, body=%wide.region_22.22_spmd.sunk | while | flops 3247706112 | bytes 45111452 | solution.py:198
  900.4 14.8 fusion.295
  928.3 14.8 fusion.295
  956.2 14.8 fusion.295
  984.1 14.8 fusion.295
  1029.1 53.4 %while.88 = (s32[]{:T(128)}, f32[4,512]{1,0:T(4,128)S(1)}, pred[512]{0:T(512)(128)(4,1)S(1)}, s32[4]{0:T(128)S(1)}, s32[]{:T(128)}, /*index=5*/bf16[4,2048,4,128...) while((s32[]{:T(128)}, f32[4,512]{1,0:T(4,128)S(1)}, ...), condition=%wide.region_21.21_spmd, body=%wide.region_19.20_spmd.sunk | while | flops 2169507840 | bytes 40941204 | solution.py:165
  1097.7 111.6 %while.89 = (s32[]{:T(128)}, f32[512,4,128]{0,2,1:T(8,128)}, bf16[4,2048,4,128]{3,1,2,0:T(8,128)(2,1)}, pred[512]{0:T(512)(128)(4,1)S(1)}, s32[4]{0:T(128)S(1)},...) while((s32[]{:T(128)}, f32[512,4,128]{0,2,1:T(8,128)}, ...), condition=%wide.region_23.23_spmd, body=%wide.region_22.22_spmd.sunk | while | flops 3247706112 | bytes 45111452 | solution.py:198
  1110.8 14.8 fusion.295
  1282.8 67.5 %all-reduce.11.cloned.1.call-done = f32[1024,1024]{1,0:T(8,128)} async-done(((f32[1024,1024]{1,0:T(8,128)}), f32[1024,1024]{1,0:T(8,128)}) %all-reduce.11.cloned.1.call-update) | async-done | bytes 4194320 | tf_op jit(solution)/shard_map/psum | solution.py:365
  1458.7 16.0 gather_fusion.3
  1483.1 35.4 %reduce-scatter.6.cloned.1.call-done = f32[4,4,2,32,128]{4,3,1,0,2:T(8,128)} async-done(((f32[4,4,32,32,128]{4,3,1,0,2:T(8,128)}), f32[4,4,2,32,128]{4,3,1,0,2:T(8,128)}) %reduce-scatter.6.cloned.1.call-update) | async-done | bytes 524304 | tf_op jit(solution)/shard_map/reduce_scatter | solution.py:380
  1531.1 185.3 %reduce-scatter.8.cloned.1.call-done = f32[3,4,2,32,352]{4,3,1,0,2:T(8,128)} async-done(((f32[3,4,32,32,352]{4,3,1,0,2:T(8,128)}), f32[3,4,2,32,352]{4,3,1,0,2:T(8,128)}) %reduce-scatter.8.cloned.1.call-update) | async-done | bytes 1081360 | tf_op jit(solution)/shard_map/reduce_scatter | solution.py:381
  (540 shorter events, 972.7 us)
Async XLA Ops:
  7.2 1515.3 %copy-start = (f32[4,4,2,128,128]{4,3,2,1,0:T(8,128)S(1)}, f32[4,4,2,128,128]{4,3,2,1,0:T(8,128)}, u32[]{:S(2)}) copy-start(f32[4,4,2,128,128]{4,3,2,1,0:T(8,128)} %param.46) | copy-start | bytes 6291460
  7.2 77.7 %all-gather.4.cloned.1.call-start = ((), (), s32[]{:S(2)}) async-start(), calls=%async_computation.3 | async-start | bytes 4456448 | tf_op jit(solution)/shard_map/all_gather | solution.py:247
  9.2 439.4 %all-reduce.5.cloned.1.call-start = ((), (), s32[]{:S(2)}) async-start(), calls=%async_computation.4 | async-start | bytes 8388608 | tf_op jit(solution)/shard_map/psum | solution.py:297
  66.5 13.8 copy-start.31
  66.5 14.3 copy-start.58
  84.3 12.8 copy-start.42
  343.2 189.2 %all-gather.6.cloned.1.call-start = ((), (), s32[]{:S(2)}) async-start(), calls=%async_computation.5 | async-start | bytes 10027008 | tf_op jit(solution)/shard_map/all_gather | solution.py:248
  345.4 379.1 %all-reduce.9.cloned.1.call-start = ((), (), s32[]{:S(2)}) async-start(), calls=%async_computation.7 | async-start | bytes 8388608 | tf_op jit(solution)/shard_map/psum | solution.py:320
  454.0 335.7 %copy-start.44 = (f32[1024]{0:T(1024)}, f32[1024]{0:T(1024)S(1)}, u32[]{:S(2)}) copy-start(f32[1024]{0:T(1024)S(1)} %get-tuple-element.1035) | copy-start | bytes 12292
  586.5 23.8 %slice-start.4 = ((s8[5767168]{0:T(1024)(128)(4,1)}), s8[4194304]{0:T(1024)(128)(4,1)S(1)}, s32[]{:S(2)}) async-start(s8[5767168]{0:T(1024)(128)(4,1)} %bitcast.457), calls=%async_computation.16 | async-start | bytes 8388608
  618.0 171.6 %all-reduce.7.cloned.1.call-start = ((), (), s32[]{:S(2)}) async-start(), calls=%async_computation.6 | async-start | bytes 4194304 | tf_op jit(solution)/shard_map/psum | solution.py:310
  625.5 724.8 %all-reduce.11.cloned.1.call-start = ((), (), s32[]{:S(2)}) async-start(), calls=%async_computation.8 | async-start | bytes 8388608 | tf_op jit(solution)/shard_map/psum | solution.py:365
  1242.2 239.5 %reduce-scatter.10.cloned.1.call-start = ((), (), s32[]{:S(2)}) async-start(), calls=%async_computation.11 | async-start | bytes 557056
  1282.8 71.7 %copy-start.51 = (f32[1024]{0:T(1024)S(1)}, f32[1024]{0:T(1024)}, u32[]{:S(2)}) copy-start(f32[1024]{0:T(1024)} %get-tuple-element.850) | copy-start | bytes 12292
  1355.6 162.9 %reduce-scatter.6.cloned.1.call-start = ((), (), s32[]{:S(2)}) async-start(), calls=%async_computation.9 | async-start | bytes 8912896 | tf_op jit(solution)/shard_map/reduce_scatter | solution.py:380
  1369.8 346.5 %reduce-scatter.8.cloned.1.call-start = ((), (), s32[]{:S(2)}) async-start(), calls=%async_computation.10 | async-start | bytes 20054016 | tf_op jit(solution)/shard_map/reduce_scatter | solution.py:381
  1475.4 47.1 %copy-start.34 = (f32[4,4,2,32,128]{4,3,2,1,0:T(8,128)S(1)}, f32[4,4,2,32,128]{4,3,2,1,0:T(8,128)}, u32[]{:S(2)}) copy-start(f32[4,4,2,32,128]{4,3,2,1,0:T(8,128)} %param.43) | copy-start | bytes 1572868
  1475.4 47.1 %copy-start.35 = (f32[4,4,2,32,128]{4,3,2,1,0:T(8,128)S(1)}, f32[4,4,2,32,128]{4,3,2,1,0:T(8,128)}, u32[]{:S(2)}) copy-start(f32[4,4,2,32,128]{4,3,2,1,0:T(8,128)} %param.44) | copy-start | bytes 1572868
  1482.5 43.5 %copy-start.53 = (f32[2,64]{1,0:T(2,128)}, f32[2,64]{1,0:T(2,128)S(1)}, u32[]{:S(2)}) copy-start(f32[2,64]{1,0:T(2,128)S(1)} %copy.210) | copy-start | bytes 1540
  1526.9 193.5 %copy-start.24 = (f32[3,4,2,32,352]{4,3,2,1,0:T(8,128)S(1)}, f32[3,4,2,32,352]{4,3,2,1,0:T(8,128)}, u32[]{:S(2)}) copy-start(f32[3,4,2,32,352]{4,3,2,1,0:T(8,128)} %param.48) | copy-start | bytes 3244036
  1717.8 12.8 copy-start.16
  1717.8 14.6 slice-start
  1730.5 15.0 copy-start.26
  1730.6 14.9 copy-start.27
  (70 other events, 373.2 us)
Sparse Core Ops, SparseCore 0:
  10.8 53.1 all-gather.3
  343.4 105.1 all-reduce.4
  451.4 80.9 all-gather.5
  618.1 106.3 all-reduce.8
  726.6 62.9 all-reduce.6
  1242.4 107.9 all-reduce.10
  1355.7 56.1 reduce-scatter.9
  1416.0 102.4 reduce-scatter.5
  1522.6 193.6 reduce-scatter.7
where the time goes:
time: 1770 us; the launch traced here: 1750 us
  waiting for transfers between devices  620 us (35%)
  matrix products  580 us (33%)
  local copies, waits for them, and re-layouts  317 us (18%)
  other arithmetic  165 us (9%)
  loops' own time  30.9 us (2%)
  blocking collectives  23.4 us (1%)
    reduce_scatter x1, waiting for transfers between devices, on_device(): lax.psum_scatter(mlp_grads, 'seq', scatter_dimension=2, tiled=True)  185 us
    dot_general x24, matrix products, memory_scores(): jnp.einsum('qhd,khd->hqk', block_queries, block_keys, preferred_element_t...  169 us
    dot_general x8, matrix products, grad_step(): jnp.einsum('hqk,khd->qhd', block_dscore, block_keys, preferred_element_ty...  119 us
    psum x1, waiting for transfers between devices, on_device(): attn_out = lax.psum(partial_attn, 'tp')  103 us
    psum x1, waiting for transfers between devices, on_device(): grad_normed_two = lax.psum(partial_two, 'tp')  90.6 us
    all_gather x1, waiting for transfers between devices, on_device(): lax.all_gather(mlp_w.astype(jnp.bfloat16), 'seq', axis=2, tiled=True)  78.4 us
    dot_general x8, matrix products, add_values(): jnp.einsum('hqk,khd->qhd', block_weights, block_values, preferred_element...  73.4 us
    psum x1, waiting for transfers between devices, on_device(): grad_normed_one = lax.psum(partial_one, 'tp')  67.5 us
  transfers between devices with their start and end apart: 9, of which 7 were waited for; matrix products, arithmetic and copies ran while one was open for 15% of the time, Pallas kernels for 0%

commit v1 on v0

v1 whole, which is shorter than its diff:
```python
import functools
import math

import jax
import jax.numpy as jnp
from jax import lax
from jax.experimental import pallas as pl
from jax.experimental.pallas import tpu as pltpu
from jax.sharding import PartitionSpec as P

norm_eps = 1e-06
adam_eps = 1e-08
beta_one = 0.9
beta_two = 0.95
learn_rate = 0.01
gain_rate = 0.02
corr_first = 1.0 - 0.9**10
corr_second = 1.0 - 0.95**10
masked_out = -1e30
rotate_precision = lax.Precision.HIGH
row_tile = 256
f32 = jnp.float32
bf16 = jnp.bfloat16
grad_type = jnp.float32


def dot_nn(left, right):
    return lax.dot_general(left, right, (((1,), (0,)), ((), ())), preferred_element_type=f32)


def dot_nt(left, right):
    return lax.dot_general(left, right, (((1,), (1,)), ((), ())), preferred_element_type=f32)


def dot_tn(left, right):
    return lax.dot_general(left, right, (((0,), (0,)), ((), ())), preferred_element_type=f32)


def cost(flops, moved, exps=0):
    return pl.CostEstimate(flops=int(flops), bytes_accessed=int(moved), transcendentals=int(exps))


def own_mask(doc_rows, doc_cols, first_row, first_col):
    shape = (doc_rows.shape[0], doc_cols.shape[1])
    rows = first_row + lax.broadcasted_iota(jnp.int32, shape, 0)
    cols = first_col + lax.broadcasted_iota(jnp.int32, shape, 1)
    return (cols <= rows) & (doc_rows == doc_cols)


def own_windows(first_row, half):
    found = []
    for offset in range(0, half, row_tile):
        start = first_row + offset
        low_key = max(0, start - half)
        found.append((offset, low_key, start + row_tile - low_key))
    return found


def late_forward(half, coef, q_ref, k_ref, v_ref, dr_ref, dc_ref, o_ref, of_ref, lse_ref):
    for offset, low_key, keys in own_windows(half, half):
        rows = pl.ds(offset, row_tile)
        cols = pl.ds(low_key, keys)
        scores = dot_nt(q_ref[rows, :], k_ref[cols, :]) * coef
        keep = own_mask(dr_ref[rows, :], dc_ref[:, cols], half + offset, low_key)
        scores = jnp.where(keep, scores, masked_out)
        top = jnp.max(scores, axis=1, keepdims=True)
        weights = jnp.exp2(scores - top)
        total = jnp.sum(weights, axis=1, keepdims=True)
        out = dot_nn(weights.astype(bf16), v_ref[cols, :]) / total
        of_ref[rows, :] = out
        o_ref[rows, :] = out.astype(bf16)
        lse_ref[rows, :] = jnp.broadcast_to(top + jnp.log2(total), (row_tile, lse_ref.shape[1]))


def late_backward(
    half, coef, scale, q_ref, k_ref, v_ref, do_ref, of_ref, lse_ref, dr_ref, dc_ref,
    dq_ref, dk_ref, dv_ref, dk_low_ref, dv_low_ref, dk_sum, dv_sum,
):
    dk_sum[...] = jnp.zeros_like(dk_sum)
    dv_sum[...] = jnp.zeros_like(dv_sum)
    for offset, low_key, keys in own_windows(half, half):
        rows = pl.ds(offset, row_tile)
        cols = pl.ds(low_key, keys)
        own_backward(
            rows, cols, half + offset, low_key, coef, q_ref, k_ref, v_ref, do_ref, of_ref, lse_ref,
            dr_ref, dc_ref, dk_sum, dv_sum,
            lambda part: dq_ref.__setitem__((rows, slice(None)), (part * scale).astype(bf16)),
        )
    dk_low_ref[...] = dk_sum[pl.ds(0, half), :]
    dv_low_ref[...] = dv_sum[pl.ds(0, half), :]
    dk_ref[...] = (dk_sum[pl.ds(half, half), :] * scale).astype(bf16)
    dv_ref[...] = dv_sum[pl.ds(half, half), :].astype(bf16)


def own_backward(
    rows, cols, first_row, first_col, coef, q_ref, k_ref, v_ref, do_ref, of_ref, lse_ref,
    dr_ref, dc_ref, dk_sum, dv_sum, put_dq,
):
    q, do = q_ref[rows, :], do_ref[rows, :]
    k, v = k_ref[cols, :], v_ref[cols, :]
    scores = dot_nt(q, k) * coef
    keep = own_mask(dr_ref[rows, :], dc_ref[:, cols], first_row, first_col)
    weights = jnp.where(keep, jnp.exp2(jnp.where(keep, scores, masked_out) - lse_ref[rows, :1]), 0.0)
    delta = jnp.sum(do.astype(f32) * of_ref[rows, :], axis=1, keepdims=True)
    dscore = (weights * (dot_nt(do, v) - delta)).astype(bf16)
    put_dq(dot_nn(dscore, k))
    dk_sum[cols, :] += dot_tn(dscore, q)
    dv_sum[cols, :] += dot_tn(weights.astype(bf16), do)


def live_steps(live, step, block_keys, sub_keys):
    left = jnp.minimum(live - step * block_keys, block_keys)
    return left // sub_keys, left % sub_keys


def each_live(info_ref, step, block_keys, sub_keys, half, body):
    live, first_len = info_ref[0], info_ref[1]
    whole, rest = live_steps(live, step, block_keys, sub_keys)

    def tiles(sub, limit):
        for offset in range(0, half, row_tile):
            if offset == 0:
                body(offset, sub, limit)
            else:
                pl.when(first_len > offset)(functools.partial(body, offset, sub, limit))

    @pl.when(live > step * block_keys)
    def _():
        def full(sub, carry):
            tiles(sub, None)
            return carry

        lax.fori_loop(0, whole, full, 0)

        @pl.when(rest > 0)
        def _():
            tiles(whole, rest)


def early_forward(
    half, coef, block_keys, sub_keys, info_ref, q_ref, k_ref, v_ref, dr_ref, dc_ref, mk_ref, mv_ref,
    o_ref, of_ref, lse_ref, top_ref, total_ref, acc_ref,
):
    step = pl.program_id(1)

    @pl.when(step == 0)
    def _():
        for offset in range(0, half, row_tile):
            rows = pl.ds(offset, row_tile)
            cols = pl.ds(0, offset + row_tile)
            scores = dot_nt(q_ref[rows, :], k_ref[cols, :]) * coef
            keep = own_mask(dr_ref[rows, :], dc_ref[:, cols], offset, 0)
            scores = jnp.where(keep, scores, masked_out)
            top = jnp.max(scores, axis=1, keepdims=True)
            weights = jnp.exp2(scores - top)
            top_ref[rows, :] = jnp.broadcast_to(top, (row_tile, 128))
            total_ref[rows, :] = jnp.broadcast_to(
                jnp.sum(weights, axis=1, keepdims=True), (row_tile, 128)
            )
            acc_ref[rows, :] = dot_nn(weights.astype(bf16), v_ref[cols, :])

    def body(offset, sub, limit):
        rows = pl.ds(offset, row_tile)
        cols = pl.ds(pl.multiple_of(sub * sub_keys, sub_keys), sub_keys)
        sees = dr_ref[rows, :] == dr0(dc_ref)
        scores = dot_nt(q_ref[rows, :], mk_ref[cols, :]) * coef
        if limit is not None:
            slots = lax.broadcasted_iota(jnp.int32, (1, sub_keys), 1)
            scores = jnp.where(slots < limit, scores, masked_out)
        old_top = top_ref[rows, :1]
        new_top = jnp.where(
            sees, jnp.maximum(old_top, jnp.max(scores, axis=1, keepdims=True)), old_top
        )
        weights = jnp.exp2(scores - jnp.where(sees, new_top, -masked_out))
        fade = jnp.exp2(old_top - new_top)
        total_ref[rows, :] = total_ref[rows, :] * fade + jnp.sum(weights, axis=1, keepdims=True)
        acc_ref[rows, :] = acc_ref[rows, :] * fade + dot_nn(weights.astype(bf16), mv_ref[cols, :])
        top_ref[rows, :] = jnp.broadcast_to(new_top, (row_tile, 128))

    each_live(info_ref, step, block_keys, sub_keys, half, body)

    @pl.when(step == pl.num_programs(1) - 1)
    def _():
        total = total_ref[...]
        out = acc_ref[...] / total[:, :1]
        of_ref[...] = out
        o_ref[...] = out.astype(bf16)
        lse_ref[...] = top_ref[...] + jnp.log2(total)


def dr0(dc_ref):
    return dc_ref[:, :1]


def early_backward(
    half, coef, scale, block_keys, sub_keys, info_ref, q_ref, k_ref, v_ref, do_ref, of_ref, lse_ref,
    dr_ref, dc_ref, dk_low_ref, dv_low_ref, mk_ref, mv_ref, dq_ref, dk_ref, dv_ref,
    dq_sum, dk_sum, dv_sum, delta_ref,
):
    step = pl.program_id(1)

    @pl.when(step == 0)
    def _():
        dk_sum[...] = dk_low_ref[...]
        dv_sum[...] = dv_low_ref[...]
        for offset in range(0, half, row_tile):
            rows = pl.ds(offset, row_tile)
            cols = pl.ds(0, offset + row_tile)
            own_backward(
                rows, cols, offset, 0, coef, q_ref, k_ref, v_ref, do_ref, of_ref, lse_ref,
                dr_ref, dc_ref, dk_sum, dv_sum,
                lambda part: dq_sum.__setitem__((rows, slice(None)), part),
            )
            delta = jnp.sum(do_ref[rows, :].astype(f32) * of_ref[rows, :], axis=1, keepdims=True)
            delta_ref[rows, :] = jnp.broadcast_to(delta, (row_tile, 128))
        dk_ref[...] = (dk_sum[...] * scale).astype(bf16)
        dv_ref[...] = dv_sum[...].astype(bf16)

    def body(offset, sub, limit):
        rows = pl.ds(offset, row_tile)
        cols = pl.ds(pl.multiple_of(sub * sub_keys, sub_keys), sub_keys)
        sees = dr_ref[rows, :] == dr0(dc_ref)
        keys = mk_ref[cols, :]
        scores = dot_nt(q_ref[rows, :], keys) * coef
        if limit is not None:
            slots = lax.broadcasted_iota(jnp.int32, (1, sub_keys), 1)
            scores = jnp.where(slots < limit, scores, masked_out)
        weights = jnp.exp2(scores - jnp.where(sees, lse_ref[rows, :1], -masked_out))
        dprob = dot_nt(do_ref[rows, :], mv_ref[cols, :])
        dscore = (weights * (dprob - delta_ref[rows, :1])).astype(bf16)
        dq_sum[rows, :] += dot_nn(dscore, keys)

    each_live(info_ref, step, block_keys, sub_keys, half, body)

    @pl.when(step == pl.num_programs(1) - 1)
    def _():
        dq_ref[...] = (dq_sum[...] * scale).astype(bf16)


class Attention:
    def __init__(self, heads, size, seg_len, mem_rows):
        self.heads, self.size, self.seg_len, self.mem_rows = heads, size, seg_len, mem_rows
        self.half = seg_len // 2
        self.scale = size ** (-0.5)
        self.coef = self.scale * math.log2(math.e)
        self.block_keys = min(2048, mem_rows)
        self.sub_keys = min(1024, self.block_keys)
        self.steps = mem_rows // self.block_keys

    def late_specs(self):
        heads, size, half, seg = self.heads, self.size, self.half, self.seg_len
        return [
            pl.BlockSpec((half, size), lambda h: (1, h)),
            pl.BlockSpec((seg, size), lambda h: (0, heads + h)),
            pl.BlockSpec((seg, size), lambda h: (0, 2 * heads + h)),
        ]

    def doc_specs_late(self):
        return [
            pl.BlockSpec((self.half, 1), lambda h: (1, 0)),
            pl.BlockSpec((1, self.seg_len), lambda h: (0, 0)),
        ]

    def head_spec(self, grid_axes):
        if grid_axes == 1:
            return pl.BlockSpec((self.half, self.size), lambda h: (0, h))
        return pl.BlockSpec((self.half, self.size), lambda h, j, info: (0, h))

    def shape(self, dtype):
        return jax.ShapeDtypeStruct((self.half, self.heads * self.size), dtype)

    def forward_late(self, projected, doc_rows, doc_cols):
        head = self.head_spec(1)
        area = self.heads * self.half * self.half * 3
        return pl.pallas_call(
            functools.partial(late_forward, self.half, self.coef),
            grid=(self.heads,),
            in_specs=self.late_specs() + self.doc_specs_late(),
            out_specs=[head, head, head],
            out_shape=[self.shape(bf16), self.shape(f32), self.shape(f32)],
            cost_estimate=cost(area * 4 * self.size, 8 * 2**20, area),
            name="late_forward",
        )(projected, projected, projected, doc_rows, doc_cols)

    def backward_late(self, projected, do, of, lse, doc_rows, doc_cols):
        head = self.head_spec(1)
        area = self.heads * self.half * self.half * 3
        return pl.pallas_call(
            functools.partial(late_backward, self.half, self.coef, self.scale),
            grid=(self.heads,),
            in_specs=self.late_specs() + [head, head, head] + self.doc_specs_late(),
            out_specs=[head] * 5,
            out_shape=[self.shape(bf16)] * 3 + [self.shape(f32)] * 2,
            scratch_shapes=[pltpu.VMEM((self.seg_len, self.size), f32)] * 2,
            cost_estimate=cost(area * 10 * self.size, 12 * 2**20, area),
            name="late_backward",
        )(projected, projected, projected, do, of, lse, doc_rows, doc_cols)

    def early_specs(self):
        heads, size, half = self.heads, self.size, self.half
        return [
            pl.BlockSpec((half, size), lambda h, j, info: (0, h)),
            pl.BlockSpec((half, size), lambda h, j, info: (0, heads + h)),
            pl.BlockSpec((half, size), lambda h, j, info: (0, 2 * heads + h)),
        ]

    def doc_specs_early(self):
        return [
            pl.BlockSpec((self.half, 1), lambda h, j, info: (0, 0)),
            pl.BlockSpec((1, self.half), lambda h, j, info: (0, 0)),
        ]

    def memory_spec(self):
        block_keys = self.block_keys

        def index(h, j, info):
            return (jnp.minimum(j, (info[0] - 1) // block_keys), h)

        return pl.BlockSpec((block_keys, self.size), index)

    def forward_early(self, info, projected, doc_rows, doc_cols, mem_keys, mem_values):
        head = self.head_spec(2)
        memory = self.memory_spec()
        area = self.heads * self.half * self.mem_rows
        return pl.pallas_call(
            functools.partial(
                early_forward, self.half, self.coef, self.block_keys, self.sub_keys
            ),
            grid_spec=pltpu.PrefetchScalarGridSpec(
                num_scalar_prefetch=1,
                grid=(self.heads, self.steps),
                in_specs=self.early_specs() + self.doc_specs_early() + [memory, memory],
                out_specs=[head, head, head],
                scratch_shapes=[pltpu.VMEM((self.half, 128), f32)] * 2
                + [pltpu.VMEM((self.half, self.size), f32)],
            ),
            out_shape=[self.shape(bf16), self.shape(f32), self.shape(f32)],
            cost_estimate=cost(area * 4 * self.size, 24 * 2**20, area),
            name="early_forward",
        )(info, projected, projected, projected, doc_rows, doc_cols, mem_keys, mem_values)

    def backward_early(
        self, info, projected, do, of, lse, doc_rows, doc_cols, dk_low, dv_low, mem_keys, mem_values
    ):
        head = self.head_spec(2)
        memory = self.memory_spec()
        area = self.heads * self.half * self.mem_rows
        return pl.pallas_call(
            functools.partial(
                early_backward, self.half, self.coef, self.scale, self.block_keys, self.sub_keys
            ),
            grid_spec=pltpu.PrefetchScalarGridSpec(
                num_scalar_prefetch=1,
                grid=(self.heads, self.steps),
                in_specs=self.early_specs()
                + [head, head, head]
                + self.doc_specs_early()
                + [head, head, memory, memory],
                out_specs=[head] * 3,
                scratch_shapes=[pltpu.VMEM((self.half, self.size), f32)] * 3
                + [pltpu.VMEM((self.half, 128), f32)],
            ),
            out_shape=[self.shape(bf16)] * 3,
            cost_estimate=cost(area * 6 * self.size, 28 * 2**20, area),
            name="early_backward",
        )(
            info, projected, projected, projected, do, of, lse, doc_rows, doc_cols, dk_low, dv_low,
            mem_keys, mem_values,
        )


def mlp_body(
    parts, *refs
):
    x_ref, parts_refs, refs = refs[0], refs[1 : 1 + parts], refs[1 + parts :]
    (dy_ref, gain_ref, wg_ref, wu_ref, wd_ref,
     hs_ref, a2_ref, u_ref, dg_ref, du_ref, mlp_ref, da_ref) = refs
    branch = parts_refs[0][...].astype(f32)
    for other in parts_refs[1:]:
        branch = branch + other[...].astype(f32)
    hs = x_ref[...].astype(f32) + branch
    hs_ref[...] = hs
    factor = lax.rsqrt(jnp.mean(hs * hs, axis=1, keepdims=True) + norm_eps)
    a2 = (hs * factor * gain_ref[...]).astype(bf16)
    a2_ref[...] = a2
    dy = dy_ref[...]
    groups = wg_ref.shape[0]
    mlp = da = None
    for g in range(groups):
        gate = dot_nn(a2, wg_ref[g])
        up = dot_nn(a2, wu_ref[g])
        grad_inner = dot_nn(dy, wd_ref[g])
        sig = 1.0 / (1.0 + jnp.exp(-gate))
        silu = gate * sig
        inner = (silu * up).astype(bf16)
        dgate = (grad_inner * up * sig * (1.0 + gate * (1.0 - sig))).astype(bf16)
        dup = (grad_inner * silu).astype(bf16)
        u_ref[g] = inner
        dg_ref[g] = dgate
        du_ref[g] = dup
        mlp_g = dot_nt(inner, wd_ref[g])
        da_g = dot_nt(dgate, wg_ref[g]) + dot_nt(dup, wu_ref[g])
        mlp = mlp_g if mlp is None else mlp + mlp_g
        da = da_g if da is None else da + da_g
    mlp_ref[...] = mlp.astype(bf16)
    da_ref[...] = da.astype(bf16)


def mlp_both(x, parts, dy, first_block, gain_row, wg, wu, wd):
    groups, width, hidden = wg.shape
    rows = parts[0].shape[0]
    tile = min(row_tile, rows)
    base = first_block * (rows // tile)
    here = pl.BlockSpec((tile, width), lambda i: (i, 0))
    there = pl.BlockSpec((tile, width), lambda i: (base + i, 0))
    weight = pl.BlockSpec((groups, width, hidden), lambda i: (0, 0, 0), pipeline_mode=pl.Buffered(1))
    wide = pl.BlockSpec((groups, tile, hidden), lambda i: (0, i, 0))
    wide_shape = jax.ShapeDtypeStruct((groups, rows, hidden), bf16)
    return pl.pallas_call(
        functools.partial(mlp_body, len(parts)),
        grid=(rows // tile,),
        in_specs=[there]
        + [here] * len(parts)
        + [there, pl.BlockSpec((1, width), lambda i: (0, 0)), weight, weight, weight],
        out_specs=[here, here, wide, wide, wide, here, here],
        out_shape=[
            jax.ShapeDtypeStruct((rows, width), f32),
            jax.ShapeDtypeStruct((rows, width), bf16),
            wide_shape,
            wide_shape,
            wide_shape,
            jax.ShapeDtypeStruct((rows, width), bf16),
            jax.ShapeDtypeStruct((rows, width), bf16),
        ],
        cost_estimate=cost(12 * rows * width * hidden * groups, 24 * 2**20, rows * hidden * groups),
        name="mlp_both",
    )(x, *parts, dy, gain_row, wg, wu, wd)


def grad_body(kinds, steps, height, pack, *refs):
    out_ref = refs[-1]
    blocks, _, _, size = out_ref.shape
    for kind in range(kinds):

        @pl.when(pl.program_id(0) // steps == kind)
        def _():
            la, lb, ra, rb = refs[4 * kind : 4 * kind + 4]
            right = [r[0] if len(r.shape) == 3 else r[...] for r in (ra, rb)]
            total = dot_tn(la[...], right[0]) + dot_tn(lb[...], right[1])
            total = total.astype(grad_type)
            for i in range(pack):
                part = total[:, i * size : (i + 1) * size]
                out_ref[:, i] = part.reshape(blocks, height, size)


def grad_call(entries, height, size, name):
    kinds = len(entries)
    rows = entries[0][2][0].shape[-2]
    width = entries[0][0][0].shape[1]
    grouped = entries[0][2][0].ndim == 3
    if grouped:
        groups, pack = entries[0][2][0].shape[0], 1
    else:
        groups = entries[0][2][0].shape[1] // size
        pack = 2 if groups % 2 == 0 else 1
    steps = groups // pack
    specs, operands = [], []
    for kind, (left, left_blocks, right) in enumerate(entries):

        def place(g, kind=kind):
            return jnp.clip(g - kind * steps, 0, steps - 1)

        for half in range(2):
            specs.append(
                pl.BlockSpec(
                    (rows, width), lambda g, b=left_blocks[half]: (b, 0), pipeline_mode=pl.Buffered(1)
                )
            )
        for half in range(2):
            if grouped:
                specs.append(pl.BlockSpec((1, rows, size), lambda g, place=place: (place(g), 0, 0)))
            else:
                specs.append(pl.BlockSpec((rows, pack * size), lambda g, place=place: (0, place(g))))
        operands += [left[0], left[1], right[0], right[1]]
    return pl.pallas_call(
        functools.partial(grad_body, kinds, steps, height, pack),
        grid=(kinds * steps,),
        in_specs=specs,
        out_specs=pl.BlockSpec((width // height, pack, height, size), lambda g: (0, g, 0, 0)),
        out_shape=jax.ShapeDtypeStruct((width // height, kinds * groups, height, size), grad_type),
        cost_estimate=cost(4 * rows * width * size * groups * kinds, 16 * 2**20),
        name=name,
    )(*operands)


def to_matrix(blocks):
    groups, block_count, height, block_width = blocks.shape
    return jnp.transpose(blocks, (1, 2, 0, 3)).reshape(block_count * height, groups * block_width)


def rotate_step(grad, first, second, left_basis, right_basis):
    turned = jnp.einsum("...ji,...jk->...ik", left_basis, grad, precision=rotate_precision)
    turned = jnp.einsum("...ik,...kl->...il", turned, right_basis, precision=rotate_precision)
    first = beta_one * first + (1.0 - beta_one) * turned
    second = beta_two * second + (1.0 - beta_two) * turned * turned
    direction = first / corr_first / (jnp.sqrt(second / corr_second) + adam_eps)
    turned_back = jnp.einsum("...ij,...jk->...ik", left_basis, direction, precision=rotate_precision)
    turned_back = jnp.einsum(
        "...ik,...lk->...il", turned_back, right_basis, precision=rotate_precision
    )
    return (-(learn_rate * turned_back), first, second)


def adam_step(grad, first, second):
    first = beta_one * first + (1.0 - beta_one) * grad
    second = beta_two * second + (1.0 - beta_two) * grad * grad
    direction = first / corr_first / (jnp.sqrt(second / corr_second) + adam_eps)
    return (-(gain_rate * direction), first, second)


def norm_backward(values, gain_row, grad_normed):
    factor = lax.rsqrt(jnp.mean(values * values, axis=-1, keepdims=True) + norm_eps)
    scaled = grad_normed * gain_row
    inner_mean = jnp.mean(scaled * values, axis=-1, keepdims=True)
    grad_values = factor * scaled - values * (factor * factor * factor) * inner_mean
    grad_gain = jnp.sum(grad_normed * values * factor, axis=0)
    return (grad_values, grad_gain)


def back_to_order(values, one_hot):
    high = lax.reduce_precision(values, 8, 7)
    low = values - high
    return dot_nt(high.astype(bf16), one_hot) + dot_nt(low.astype(bf16), one_hot)


def on_device(
    tp_size,
    tokens,
    cotangent,
    mem_keys,
    mem_values,
    doc_ids,
    mem_len,
    owner_perm,
    gain_w,
    gain_m,
    gain_v,
    attn_w,
    attn_m,
    attn_v,
    attn_left,
    attn_right,
    mlp_w,
    mlp_m,
    mlp_v,
    mlp_left,
    mlp_right,
):
    def share(part):
        part = part.astype(bf16)
        if tp_size == 2:
            other = lax.ppermute(part, "tp", [(0, 1), (1, 0)])
            return [part, other]
        return [lax.psum(part, "tp")]

    def total(parts):
        out = parts[0].astype(f32)
        for other in parts[1:]:
            out = out + other.astype(f32)
        return out

    gain_stored = lax.all_gather(gain_w, "seq", axis=1, tiled=True)
    attn_low = lax.all_gather(attn_w.astype(bf16), "seq", axis=2, tiled=True)
    mlp_low = lax.all_gather(mlp_w.astype(bf16), "seq", axis=2, tiled=True)
    kinds, head_count, block_total, block_height, head_size = attn_low.shape
    group_count, hidden = mlp_low.shape[1], mlp_low.shape[4]
    seg_len, width = tokens.shape
    half = seg_len // 2
    width_heads = head_count * head_size

    order = (
        owner_perm[:, None] * block_height + jnp.arange(block_height, dtype=jnp.int32)[None, :]
    ).reshape(width)
    one_hot = (jnp.arange(width, dtype=jnp.int32)[:, None] == order[None, :]).astype(bf16)
    inverse = (
        jnp.zeros((block_total,), jnp.int32)
        .at[owner_perm]
        .set(jnp.arange(block_total, dtype=jnp.int32))
    )
    gain_pair = gain_stored.reshape(2, block_total, block_height)[:, owner_perm].reshape(2, width)
    x_low = dot_nn(tokens, one_hot).astype(bf16)
    dy_low = dot_nn(cotangent, one_hot).astype(bf16)

    doc_row = doc_ids
    doc_col = doc_ids.reshape(seg_len, 1)
    first_len = jnp.sum((doc_ids[0] == doc_ids[0, 0]).astype(jnp.int32))
    info = jnp.stack([mem_len[0], first_len]).astype(jnp.int32)
    attention = Attention(head_count, head_size, seg_len, mem_keys.shape[0])

    weight_qkv = jnp.concatenate([to_matrix(attn_low[i]) for i in range(3)], axis=1)
    weight_out = to_matrix(attn_low[3])
    mlp_mats = mlp_low.reshape(3, group_count, width, hidden)

    resid = x_low.astype(f32)
    factor_one = lax.rsqrt(jnp.mean(resid * resid, axis=-1, keepdims=True) + norm_eps)
    acts_one = (resid * factor_one * gain_pair[0]).astype(bf16)
    projected = dot_nn(acts_one, weight_qkv).astype(bf16)
    keys_new = projected[:, width_heads : 2 * width_heads]
    values_new = projected[:, 2 * width_heads :]

    o_late, of_late, lse_late = attention.forward_late(projected, doc_col, doc_row)
    attn_late = share(dot_nt(o_late, weight_out))
    o_early, of_early, lse_early = attention.forward_early(
        info, projected, doc_col, doc_row, mem_keys, mem_values
    )
    attn_early = share(dot_nt(o_early, weight_out))

    gain_two = gain_pair[1:2]
    hs_late, a2_late, u_late, dg_late, du_late, mlp_late, da_late = mlp_both(
        x_low, attn_late, dy_low, 1, gain_two, mlp_mats[0], mlp_mats[1], mlp_mats[2]
    )
    da_late = share(da_late)
    hs_early, a2_early, u_early, dg_early, du_early, mlp_early, da_early = mlp_both(
        x_low, attn_early, dy_low, 0, gain_two, mlp_mats[0], mlp_mats[1], mlp_mats[2]
    )
    da_early = share(da_early)
    mlp_late = share(mlp_late)
    mlp_early = share(mlp_early)

    def scatter(grads, kinds):
        owned = lax.psum_scatter(grads, "seq", scatter_dimension=0, tiled=True).astype(f32)
        own_blocks, _, height, size = owned.shape
        owned = owned.reshape(own_blocks, kinds, grads.shape[1] // kinds, height, size)
        return jnp.transpose(owned, (1, 2, 0, 3, 4))

    a2_pair = (a2_early, a2_late)
    mlp_grads = grad_call(
        [
            (a2_pair, (0, 0), (dg_early, dg_late)),
            (a2_pair, (0, 0), (du_early, du_late)),
            ((dy_low, dy_low), (0, 1), (u_early, u_late)),
        ],
        block_height,
        hidden,
        "mlp_grads",
    )
    mlp_grad = scatter(mlp_grads, 3)

    def hidden_grad(hs, dy, parts):
        grad, grad_gain = norm_backward(hs, gain_pair[1], total(parts))
        return dy.astype(f32) + grad, grad_gain

    dh_late, gain_late = hidden_grad(hs_late, dy_low[half:], da_late)
    dhr_late = dh_late.astype(bf16)
    do_late = dot_nn(dhr_late, weight_out).astype(bf16)
    dq_late, dk_late, dv_late, dk_low, dv_low = attention.backward_late(
        projected, do_late, of_late, lse_late, doc_col, doc_row
    )
    dproj_late = jnp.concatenate([dq_late, dk_late, dv_late], axis=1)
    one_late = share(dot_nt(dproj_late, weight_qkv))

    dh_early, gain_early = hidden_grad(hs_early, dy_low[:half], da_early)
    dhr_early = dh_early.astype(bf16)
    do_early = dot_nn(dhr_early, weight_out).astype(bf16)
    out_grads = grad_call(
        [((dhr_early, dhr_late), (0, 0), (o_early, o_late))], block_height, head_size, "out_grads"
    )
    out_grad = scatter(out_grads, 1)[0]
    dq_early, dk_early, dv_early = attention.backward_early(
        info, projected, do_early, of_early, lse_early, doc_col, doc_row, dk_low, dv_low,
        mem_keys, mem_values,
    )
    dproj_early = jnp.concatenate([dq_early, dk_early, dv_early], axis=1)
    one_early = share(dot_nt(dproj_early, weight_qkv))
    acts_pair = (acts_one, acts_one)
    qkv_grads = grad_call(
        [
            (acts_pair, (0, 1), (dq_early, dq_late)),
            (acts_pair, (0, 1), (dk_early, dk_late)),
            (acts_pair, (0, 1), (dv_early, dv_late)),
        ],
        block_height,
        head_size,
        "qkv_grads",
    )
    qkv_grad = scatter(qkv_grads, 3)
    attn_grad = jnp.concatenate([qkv_grad, out_grad[None]], axis=0)

    hidden_out = jnp.concatenate(
        [hs_early + total(mlp_early), hs_late + total(mlp_late)], axis=0
    )
    block_out = back_to_order(hidden_out, one_hot)

    grad_one = jnp.concatenate([total(one_early), total(one_late)], axis=0)
    grad_tokens, gain_first = norm_backward(resid, gain_pair[0], grad_one)
    grad_in = jnp.concatenate([dh_early, dh_late], axis=0) + grad_tokens
    input_grad = back_to_order(grad_in, one_hot)

    gain_grads = jnp.stack([gain_first, gain_early + gain_late])
    gain_grads = gain_grads.reshape(2, block_total, block_height)[:, inverse].reshape(2, width)
    gain_grad = lax.psum_scatter(gain_grads, "seq", scatter_dimension=1, tiled=True)

    mlp_new = rotate_step(mlp_grad, mlp_m, mlp_v, mlp_left, mlp_right)
    qkv_new = rotate_step(qkv_grad, attn_m[:3], attn_v[:3], attn_left[:3], attn_right[:3])
    out_new = rotate_step(out_grad, attn_m[3], attn_v[3], attn_left[3], attn_right[3])
    gain_new = adam_step(gain_grad, gain_m, gain_v)
    return (
        block_out,
        input_grad,
        keys_new,
        values_new,
        attn_grad,
        mlp_grad,
        gain_grad,
        jnp.concatenate([qkv_new[0], out_new[0][None]], axis=0),
        jnp.concatenate([qkv_new[1], out_new[1][None]], axis=0),
        qkv_new[2],
        out_new[2],
        mlp_w + mlp_new[0],
        mlp_new[1],
        mlp_new[2],
        gain_new[0],
        gain_new[1],
        gain_new[2],
    )


def solution(mesh):
    in_specs = (
        P("seq", None),
        P("seq", None),
        P("seq", "tp"),
        P("seq", "tp"),
        P("seq", None),
        P("seq"),
        P(),
        P(None, "seq"),
        P(None, "seq"),
        P(None, "seq"),
        P(None, "tp", "seq", None, None),
        P(None, "tp", "seq", None, None),
        P(None, "tp", "seq", None, None),
        P(None, "tp", "seq", None, None),
        P(None, "tp", "seq", None, None),
        P(None, "tp", "seq", None, None),
        P(None, "tp", "seq", None, None),
        P(None, "tp", "seq", None, None),
        P(None, "tp", "seq", None, None),
        P(None, "tp", "seq", None, None),
    )
    out_specs = (
        P("seq", None),
        P("seq", None),
        P("seq", "tp"),
        P("seq", "tp"),
        P(None, "tp", "seq", None, None),
        P(None, "tp", "seq", None, None),
        P(None, "seq"),
        P(None, "tp", "seq", None, None),
        P(None, "tp", "seq", None, None),
        P(None, "tp", "seq", None, None),
        P("tp", "seq", None, None),
        P(None, "tp", "seq", None, None),
        P(None, "tp", "seq", None, None),
        P(None, "tp", "seq", None, None),
        P(None, "seq"),
        P(None, "seq"),
        P(None, "seq"),
    )
    return jax.shard_map(
        functools.partial(on_device, mesh.shape["tp"]), mesh=mesh, in_specs=in_specs, out_specs=out_specs, check_vma=False
    )
```

time: 1770 us -> 798 us (0.45)
  matrix products: 580 us -> 65.9 us
  local copies, waits for them, and re-layouts: 317 us -> 31 us
  waiting for transfers between devices: 620 us -> 464 us
  Pallas kernels: 0 us -> 153 us
  other arithmetic: 165 us -> 27.3 us
  loops' own time: 30.9 us -> 0 us
    dot_general x82 -> x25, matrix products: 580 us -> 65.9 us  [the longest x8 27.8 us: dot_nt(): lax.dot_general(left, right, (((1,), (1,)), ((), ())), preferred_element_...]
    psum x4 -> x0, waiting for transfers between devices: 321 us -> none  [the longest x1 103 us: on_device(): attn_out = lax.psum(partial_attn, 'tp')]
    pallas_call x0 -> x9, Pallas kernels: none -> 153 us  [the longest x2 42.7 us: mlp_both(): pl.pallas_call(functools.partial(mlp_body, len(parts)), grid=(rows // til...]
    reduce_scatter x2 -> x3, waiting for transfers between devices: 221 us -> 337 us  [scatter(): lax.psum_scatter(grads, 'seq', scatter_dimension=0, tiled=True).astype(f32)]
    reshape x20 -> x5, local copies, waits for them, and re-layouts: 108 us -> 3.67 us  [the longest x2 2.53 us: scatter(): owned.reshape(own_blocks, kinds, grads.shape[1] // kinds, height, size)]
    ppermute x0 -> x8, waiting for transfers between devices: none -> 80.7 us  [share(): other = lax.ppermute(part, 'tp', [(0, 1), (1, 0)])]
    unnamed x124 -> x111, local copies, waits for them, and re-layouts: 53.7 us -> 7.53 us
    reduce_sum x12 -> x3, other arithmetic: 41.7 us -> 1.71 us  [the longest x1 1.28 us: on_device(): first_len = jnp.sum((doc_ids[0] == doc_ids[0, 0]).astype(jnp.int32))]
  transfers between devices with their start and end apart: 9 -> 14, of which waited for: 7 -> 10; matrix products, arithmetic and copies ran while one was open for 15% -> 11% of each run, Pallas kernels for 0% -> 18%
where the time goes in v1:
time: 798 us; the launch traced here: 789 us
  waiting for transfers between devices  464 us (58%)
  Pallas kernels  153 us (19%)
  matrix products  65.9 us (8%)
  local copies, waits for them, and re-layouts  31 us (4%)
  other arithmetic  27.3 us (3%)
  blocking collectives  23.2 us (3%)
  between operations  15.9 us (2%)
  starting transfers between devices  8.62 us (1%)
    reduce_scatter x3, waiting for transfers between devices, scatter(): lax.psum_scatter(grads, 'seq', scatter_dimension=0, tiled=True).astype(f32)  337 us
    ppermute x8, waiting for transfers between devices, share(): other = lax.ppermute(part, 'tp', [(0, 1), (1, 0)])  80.7 us
    pallas_call x2, Pallas kernels, mlp_both(): pl.pallas_call(functools.partial(mlp_body, len(parts)), grid=(rows // til...  42.7 us
    pallas_call x3, Pallas kernels, grad_call(): pl.pallas_call(functools.partial(grad_body, kinds, steps, height, pack),...  38.9 us
    pallas_call x1, Pallas kernels, forward_early(): pl.pallas_call(functools.partial(early_forward, self.half, self.coef, sel...  28.9 us
    dot_general x8, matrix products, dot_nt(): lax.dot_general(left, right, (((1,), (1,)), ((), ())), preferred_element_...  27.8 us
    pallas_call x1, Pallas kernels, backward_early(): pl.pallas_call(functools.partial(early_backward, self.half, self.coef, se...  27.1 us
    all_gather x1, blocking collectives, on_device(): gain_stored = lax.all_gather(gain_w, 'seq', axis=1, tiled=True)  23.2 us
  transfers between devices with their start and end apart: 14, of which 10 were waited for; matrix products, arithmetic and copies ran while one was open for 11% of the time, Pallas kernels for 18%

profile of v1, /device:TPU:0, one launch (start us, length us, event | category | flops | bytes accessed | tf_op | source)
XLA Modules:
  0.0 788.6 jit_solution(1201551981543892144)
XLA Ops:
  12.9 23.2 %all-gather = f32[16,64,2]{1,2,0:T(2,128)S(1)} all-gather(f32[1,64,2]{1,2,0:T(2,128)S(1)} %bitcast.156), channel_id=1, replica_groups=mesh['seq'=16,'tp'=2] {'seq'}, dimensions={0}, use_global_device_ids=true | all-gather | bytes 8704 | tf_op jit(solution)/shard_map/all_gather | solution.py:572
  45.8 18.4 %all-gather.4.cloned.1.call-done = bf16[4,4,32,32,128]{4,3,2,1,0:T(8,128)(2,1)} async-done(((bf16[4,4,2,32,128]{4,3,2,1,0:T(8,128)(2,1)}), bf16[4,4,32,32,128]{4,3,2,1,0:T(8,128)(2,1)}) %all-gather.4.cloned.1.call-update) | async-done | bytes 4194320 | tf_op jit(solution)/shard_map/all_gather | solution.py:573
  72.9 5.0 convolution_convert_fusion.q_ref.k_ref.v_ref
  77.9 28.9 %early_forward.1 = (bf16[512,512]{1,0:T(8,128)(2,1)}, f32[512,512]{1,0:T(8,128)}, f32[512,512]{1,0:T(8,128)}) custom-call(s32[2]{0:T(128)} %pad_add_fusion.info_ref, bf16[1024,1536]{1,0:T(8,128)(2,1)} %convolution_convert_fusion.q_ref.k_ref.v_ref, bf16[1024,1536]{1,0:T(8,128)(2,1)} %convolution_convert_fusion.q_ref.k_ref.v_ref, ...), custom_call_target="tpu_custom_call" | custom-call | flops 8589934592 | bytes 25165824 | tf_op jit(solution)/shard_map/early_forward/pallas_call | solution.py:325
  115.6 6.9 late_forward.1
  125.8 20.7 %all-gather.6.cloned.1.call-done = bf16[3,4,32,32,352]{4,3,2,1,0:T(8,128)(2,1)} async-done(((bf16[3,4,2,32,352]{4,3,2,1,0:T(8,128)(2,1)}), bf16[3,4,32,32,352]{4,3,2,1,0:T(8,128)(2,1)}) %all-gather.6.cloned.1.call-update) | async-done | bytes 8650768 | tf_op jit(solution)/shard_map/all_gather | solution.py:574
  146.5 6.6 fusion.136
  153.1 21.5 %mlp_both.2 = (f32[512,1024]{1,0:T(8,128)}, bf16[512,1024]{1,0:T(8,128)(2,1)}, bf16[4,512,352]{2,1,0:T(8,128)(2,1)}, bf16[4,512,352]{2,1,0:T(8,128)(2,1)}, bf16[...) custom-call(bf16[1024,1024]{1,0:T(8,128)(2,1)} %copy-done.3, ...), custom_call_target="tpu_custom_call" | custom-call | flops 8858370048 | bytes 25165824 | tf_op jit(solution)/shard_map/mlp_both/pallas_call | solution.py:419
  176.2 21.2 %mlp_both.3 = (f32[512,1024]{1,0:T(8,128)}, bf16[512,1024]{1,0:T(8,128)(2,1)}, bf16[4,512,352]{2,1,0:T(8,128)(2,1)}, bf16[4,512,352]{2,1,0:T(8,128)(2,1)}, bf16[...) custom-call(bf16[1024,1024]{1,0:T(8,128)(2,1)} %copy-done.3, ...), custom_call_target="tpu_custom_call" | custom-call | flops 8858370048 | bytes 25165824 | tf_op jit(solution)/shard_map/mlp_both/pallas_call | solution.py:419
  200.6 23.2 %collective-permute-done.5 = bf16[512,1024]{1,0:T(8,128)(2,1)} collective-permute-done((bf16[512,1024]{1,0:T(8,128)(2,1)}, bf16[512,1024]{1,0:T(8,128)(2,1)}, u32[]{:S(2)}, u32[]{:S(2)}) %collective-permute-start.5) | collective-permute-done | bytes 1048608 | tf_op jit(solution)/shard_map/ppermute | solution.py:562
  227.4 18.8 %collective-permute-done.3 = bf16[512,1024]{1,0:T(8,128)(2,1)S(1)} collective-permute-done((bf16[512,1024]{1,0:T(8,128)(2,1)}, bf16[512,1024]{1,0:T(8,128)(2,1)S(1)}, u32[]{:S(2)}, u32[]{:S(2)}) %collective-permute-start.3) | collective-permute-done | bytes 1048608 | tf_op jit(solution)/shard_map/ppermute | solution.py:562
  246.2 21.5 %collective-permute-done.1 = bf16[512,1024]{1,0:T(8,128)(2,1)S(1)} collective-permute-done((bf16[512,1024]{1,0:T(8,128)(2,1)}, bf16[512,1024]{1,0:T(8,128)(2,1)S(1)}, u32[]{:S(2)}, u32[]{:S(2)}) %collective-permute-start.1) | collective-permute-done | bytes 1048608 | tf_op jit(solution)/shard_map/ppermute | solution.py:562
  267.7 5.6 fusion.134
  275.8 8.3 %late_backward.1 = (bf16[512,512]{1,0:T(8,128)(2,1)}, bf16[512,512]{1,0:T(8,128)(2,1)}, bf16[512,512]{1,0:T(8,128)(2,1)}, f32[512,512]{1,0:T(8,128)}, f32[512,512]{1,0:T(8,128)}) custom-call(bf16[1024,1536]{1,0:T(8,128)(2,1)} %convolution_convert_fusion.q_ref.k_ref.v_ref, bf16[1024,1536]{1,0:T(8,128)(2,1)} %convolution_convert_fusion.q_ref.k_ref.v_ref, ...), custom_call_target="tpu_custom_call" | custom-call | flops 4026531840 | bytes 12582912 | tf_op jit(solution)/shard_map/late_backward/pallas_call | solution.py:288
  291.5 27.1 %early_backward.1 = (bf16[512,512]{1,0:T(8,128)(2,1)}, bf16[512,512]{1,0:T(8,128)(2,1)}, bf16[512,512]{1,0:T(8,128)(2,1)}) custom-call(s32[2]{0:T(128)} %pad_add_fusion.info_ref, bf16[1024,1536]{1,0:T(8,128)(2,1)} %convolution_convert_fusion.q_ref.k_ref.v_ref, bf16[1024,1536]{1,0:T(8,128)(2,1)} %convolution_convert_fusion.q_ref.k_ref.v_ref, ...), custom_call_target="tpu_custom_call" | custom-call | flops 12884901888 | bytes 29360128 | tf_op jit(solution)/shard_map/early_backward/pallas_call | solution.py:348
  325.2 17.2 %collective-permute-done.6 = bf16[512,1024]{1,0:T(8,128)(2,1)} collective-permute-done((bf16[512,1024]{1,0:T(8,128)(2,1)S(1)}, bf16[512,1024]{1,0:T(8,128)(2,1)}, u32[]{:S(2)}, u32[]{:S(2)}) %collective-permute-start.6) | collective-permute-done | bytes 1048608 | tf_op jit(solution)/shard_map/ppermute | solution.py:562
  351.9 11.7 %qkv_grads.1 = f32[32,12,32,128]{3,2,1,0:T(8,128)} custom-call(bf16[1024,1024]{1,0:T(8,128)(2,1)} %copy-done.2, bf16[1024,1024]{1,0:T(8,128)(2,1)} %copy-done.2, bf16[512,512]{1,0:T(8,128)(2,1)} %get-tuple-element.59.refs_2_, bf16[512,512]{1,0:T(8,128)(2,1)} %get-tuple-element.62.refs_3_, bf16[1024,1024]{1,0:T(8,128)(2,1)} %copy-done.2, ...), custom_call_target="tpu_custom_call" | custom-call | flops 3221225472 | bytes 16777216 | tf_op jit(solution)/shard_map/qkv_grads/pallas_call | solution.py:485
  363.6 22.8 %mlp_grads.1 = f32[32,12,32,352]{3,2,1,0:T(8,128)} custom-call(bf16[512,1024]{1,0:T(8,128)(2,1)} %get-tuple-element.65.refs_0_.refs_4_, bf16[512,1024]{1,0:T(8,128)(2,1)} %get-tuple-element.66.refs_1_.refs_5_, bf16[4,512,352]{2,1,0:T(8,128)(2,1)} %get-tuple-element.67.refs_2_, bf16[4,512,352]{2,1,0:T(8,128)(2,1)} %get-tuple-element.68.refs_3_, ...), custom_call_target="tpu_custom_call" | custom-call | flops 8858370048 | bytes 16777216 | tf_op jit(solution)/shard_map/mlp_grads/pallas_call | solution.py:485
  405.9 7.4 reduce-scatter.13.cloned.1.call-done
  414.7 63.0 %reduce-scatter.9.cloned.1.call-done = f32[2,4,32,128]{3,2,1,0:T(8,128)} async-done(((f32[32,4,32,128]{3,2,1,0:T(8,128)}), f32[2,4,32,128]{3,2,1,0:T(8,128)}) %reduce-scatter.9.cloned.1.call-update) | async-done | bytes 131088 | tf_op jit(solution)/shard_map/reduce_scatter | solution.py:631
  481.2 84.3 %reduce-scatter.7.cloned.1.call-done = f32[2,12,32,128]{3,2,1,0:T(8,128)} async-done(((f32[32,12,32,128]{3,2,1,0:T(8,128)}), f32[2,12,32,128]{3,2,1,0:T(8,128)}) %reduce-scatter.7.cloned.1.call-update) | async-done | bytes 393232 | tf_op jit(solution)/shard_map/reduce_scatter | solution.py:631
  573.4 189.3 %reduce-scatter.11.cloned.1.call-done = f32[2,12,32,352]{3,2,1,0:T(8,128)} async-done(((f32[32,12,32,352]{3,2,1,0:T(8,128)}), f32[2,12,32,352]{3,2,1,0:T(8,128)}) %reduce-scatter.11.cloned.1.call-update) | async-done | bytes 1081360 | tf_op jit(solution)/shard_map/reduce_scatter | solution.py:631
  765.0 7.5 multiply_add_fusion
  774.7 6.9 fusion.52
  (213 shorter events, 105.8 us)
Async XLA Ops:
  7.2 56.9 %all-gather.4.cloned.1.call-start = ((), (), s32[]{:S(2)}) async-start(), calls=%async_computation.4 | async-start | bytes 4456448 | tf_op jit(solution)/shard_map/all_gather | solution.py:573
  9.2 137.3 %all-gather.6.cloned.1.call-start = ((), (), s32[]{:S(2)}) async-start(), calls=%async_computation.5 | async-start | bytes 10027008 | tf_op jit(solution)/shard_map/all_gather | solution.py:574
  11.5 401.8 %reduce-scatter.13.cloned.1.call-start = ((), (), s32[]{:S(2)}) async-start(), calls=%async_computation.9 | async-start | bytes 557056
  70.6 51.9 %copy-start.29 = (bf16[32,32,4,128]{3,2,1,0:T(4,128)(2,1)}, bf16[32,32,4,128]{3,2,1,0:T(4,128)(2,1)S(1)}, u32[]{:S(2)}) copy-start(bf16[32,32,4,128]{3,2,1,0:T(4,128)(2,1)S(1)} %copy.82) | copy-start | bytes 3145732
  109.7 43.4 %collective-permute-start = (bf16[512,1024]{1,0:T(8,128)(2,1)}, bf16[512,1024]{1,0:T(8,128)(2,1)}, u32[]{:S(2)}, u32[]{:S(2)}) collective-permute-start(bf16[512,1024]{1,0:T(8,128)(2,1)} %convolution_convert_fusion.2.refs_1_), channel_id=1, source_target_pairs={{0,1},{1,0},{2,3},{3,2},{4,5},{5,4},{6,7},{7,6},{8,9},{9,8},{10,11... | collective-permute-start | bytes 3145736 | tf_op jit(solution)/shard_map/ppermute | solution.py:562
  125.3 50.9 %collective-permute-start.2 = (bf16[512,1024]{1,0:T(8,128)(2,1)}, bf16[512,1024]{1,0:T(8,128)(2,1)}, u32[]{:S(2)}, u32[]{:S(2)}) collective-permute-start(bf16[512,1024]{1,0:T(8,128)(2,1)} %convolution_convert_fusion.1.refs_1_), channel_id=1, source_target_pairs={{0,1},{1,0},{2,3},{3,2},{4,5},{5,4},{6,7},{7,6},{8,9},{9,8},{10,11... | collective-permute-start | bytes 3145736 | tf_op jit(solution)/shard_map/ppermute | solution.py:562
  174.6 25.9 %collective-permute-start.4 = (bf16[512,1024]{1,0:T(8,128)(2,1)}, bf16[512,1024]{1,0:T(8,128)(2,1)}, u32[]{:S(2)}, u32[]{:S(2)}) collective-permute-start(bf16[512,1024]{1,0:T(8,128)(2,1)} %get-tuple-element.51), channel_id=1, source_target_pairs={{0,1},{1,0},{2,3},{3,2},{4,5},{5,4},{6,7},{7,6},{8,9},{9,8},{10,11... | collective-permute-start | bytes 3145736 | tf_op jit(solution)/shard_map/ppermute | solution.py:562
  176.2 47.6 %copy-start.20 = (bf16[512,1024]{1,0:T(8,128)(2,1)S(1)}, bf16[512,1024]{1,0:T(8,128)(2,1)}, u32[]{:S(2)}) copy-start(bf16[512,1024]{1,0:T(8,128)(2,1)} %get-tuple-element.51) | copy-start | bytes 3145732
  197.4 26.4 %collective-permute-start.5 = (bf16[512,1024]{1,0:T(8,128)(2,1)}, bf16[512,1024]{1,0:T(8,128)(2,1)}, u32[]{:S(2)}, u32[]{:S(2)}) collective-permute-start(bf16[512,1024]{1,0:T(8,128)(2,1)} %get-tuple-element.52), channel_id=1, source_target_pairs={{0,1},{1,0},{2,3},{3,2},{4,5},{5,4},{6,7},{7,6},{8,9},{9,8},{10,11... | collective-permute-start | bytes 3145736 | tf_op jit(solution)/shard_map/ppermute | solution.py:562
  198.1 48.1 %collective-permute-start.3 = (bf16[512,1024]{1,0:T(8,128)(2,1)}, bf16[512,1024]{1,0:T(8,128)(2,1)S(1)}, u32[]{:S(2)}, u32[]{:S(2)}) collective-permute-start(bf16[512,1024]{1,0:T(8,128)(2,1)} %get-tuple-element.50), channel_id=1, source_target_pairs={{0,1},{1,0},{2,3},{3,2},{4,5},{5,4},{6,7},{7,6},{8,9},{9,8},{10,11... | collective-permute-start | bytes 3145736 | tf_op jit(solution)/shard_map/ppermute | solution.py:562
  199.6 68.1 %collective-permute-start.1 = (bf16[512,1024]{1,0:T(8,128)(2,1)}, bf16[512,1024]{1,0:T(8,128)(2,1)S(1)}, u32[]{:S(2)}, u32[]{:S(2)}) collective-permute-start(bf16[512,1024]{1,0:T(8,128)(2,1)} %get-tuple-element.47), channel_id=1, source_target_pairs={{0,1},{1,0},{2,3},{3,2},{4,5},{5,4},{6,7},{7,6},{8,9},{9,8},{10,11... | collective-permute-start | bytes 3145736 | tf_op jit(solution)/shard_map/ppermute | solution.py:562
  223.8 43.8 %copy-start.9 = (bf16[1024,1024]{1,0:T(8,128)(2,1)S(1)}, bf16[1024,1024]{1,0:T(8,128)(2,1)}, u32[]{:S(2)}) copy-start(bf16[1024,1024]{1,0:T(8,128)(2,1)} %convert_bitcast_fusion.refs_3_.refs_8_.refs_9_) | copy-start | bytes 6291460
  223.8 43.8 %copy-start.21 = (bf16[512,1024]{1,0:T(8,128)(2,1)S(1)}, bf16[512,1024]{1,0:T(8,128)(2,1)}, u32[]{:S(2)}) copy-start(bf16[512,1024]{1,0:T(8,128)(2,1)} %get-tuple-element.51) | copy-start | bytes 3145732
  288.4 35.1 %collective-permute-start.7 = (bf16[512,1024]{1,0:T(8,128)(2,1)S(1)}, bf16[512,1024]{1,0:T(8,128)(2,1)}, u32[]{:S(2)}, u32[]{:S(2)}) collective-permute-start(bf16[512,1024]{1,0:T(8,128)(2,1)S(1)} %fusion.41), channel_id=1, source_target_pairs={{0,1},{1,0},{2,3},{3,2},{4,5},{5,4},{6,7},{7,6},{8,9},{9,8},{10,11... | collective-permute-start | bytes 3145736 | tf_op jit(solution)/shard_map/ppermute | solution.py:562
  322.8 19.6 %collective-permute-start.6 = (bf16[512,1024]{1,0:T(8,128)(2,1)S(1)}, bf16[512,1024]{1,0:T(8,128)(2,1)}, u32[]{:S(2)}, u32[]{:S(2)}) collective-permute-start(bf16[512,1024]{1,0:T(8,128)(2,1)S(1)} %fusion.44), channel_id=1, source_target_pairs={{0,1},{1,0},{2,3},{3,2},{4,5},{5,4},{6,7},{7,6},{8,9},{9,8},{10,11... | collective-permute-start | bytes 3145736 | tf_op jit(solution)/shard_map/ppermute | solution.py:562
  347.3 130.4 %reduce-scatter.9.cloned.1.call-start = ((), (), s32[]{:S(2)}) async-start(), calls=%async_computation.7 | async-start | bytes 2228224 | tf_op jit(solution)/shard_map/reduce_scatter | solution.py:631
  351.8 213.7 %reduce-scatter.7.cloned.1.call-start = ((), (), s32[]{:S(2)}) async-start(), calls=%async_computation.6 | async-start | bytes 6684672 | tf_op jit(solution)/shard_map/reduce_scatter | solution.py:631
  363.6 399.1 %reduce-scatter.11.cloned.1.call-start = ((), (), s32[]{:S(2)}) async-start(), calls=%async_computation.8 | async-start | bytes 20054016 | tf_op jit(solution)/shard_map/reduce_scatter | solution.py:631
  401.4 77.6 %copy-start.13 = (f32[4,4,2,128,128]{4,3,2,1,0:T(8,128)S(1)}, f32[4,4,2,128,128]{4,3,2,1,0:T(8,128)}, u32[]{:S(2)}) copy-start(f32[4,4,2,128,128]{4,3,2,1,0:T(8,128)} %param.34) | copy-start | bytes 6291460
  401.4 77.9 %copy-start.34 = (f32[4,4,2,32,128]{4,3,2,1,0:T(8,128)S(1)}, f32[4,4,2,32,128]{4,3,2,1,0:T(8,128)}, u32[]{:S(2)}) copy-start(f32[4,4,2,32,128]{4,3,2,1,0:T(8,128)} %param.31) | copy-start | bytes 1572868
  401.4 77.9 %copy-start.35 = (f32[4,4,2,32,128]{4,3,2,1,0:T(8,128)S(1)}, f32[4,4,2,32,128]{4,3,2,1,0:T(8,128)}, u32[]{:S(2)}) copy-start(f32[4,4,2,32,128]{4,3,2,1,0:T(8,128)} %param.32) | copy-start | bytes 1572868
  414.1 154.1 %copy-start.43 = (f32[2,64]{1,0:T(2,128)}, f32[2,64]{1,0:T(2,128)S(1)}, u32[]{:S(2)}) copy-start(f32[2,64]{1,0:T(2,128)S(1)} %copy.101) | copy-start | bytes 1540
  479.4 89.5 %copy-start.41 = (f32[4,2,32,128]{3,2,1,0:T(8,128)}, f32[4,2,32,128]{3,2,1,0:T(8,128)S(1)}, u32[]{:S(2)}) copy-start(f32[4,2,32,128]{3,2,1,0:T(8,128)S(1)} %get-tuple-element.106) | copy-start | bytes 393220
  571.7 192.5 %copy-start.39 = (f32[3,4,2,32,32]{4,3,2,1,0:T(8,128)S(1)}, f32[3,4,2,32,32]{4,3,2,1,0:T(8,128)}, u32[]{:S(2)}) copy-start(f32[3,4,2,32,32]{4,3,2,1,0:T(8,128)} %param.38) | copy-start | bytes 294916
  (43 other events, 452.1 us)
Sparse Core Ops, SparseCore 0:
  10.8 53.3 all-gather.3
  67.0 79.4 all-gather.5
  347.4 65.7 reduce-scatter.12
  416.8 60.8 reduce-scatter.8
  481.5 83.9 reduce-scatter.6
  569.5 193.1 reduce-scatter.10
